TPU v7x, 32 devices: a whole 2x2x4 slice. The times are simulated.
32 devices in a mesh: dp: 32 (over z, y, x, core), tensor: 1.
Axes of the slice: x: 2, y: 2, z: 4, core: 2. Of those that a mesh axis runs over, the one named last changes fastest.
Arguments:
- grad_codes: bfloat16 [4, 32, 32, 18432], P(None, 'dp', None, 'tensor'), may hold values from -448 to 448
- exponents: int32 [4, 32, 16], P(None, 'dp'), may hold values from 7 to 10
- accumulated: bfloat16 [32, 18432], P('dp', 'tensor'), may hold values from -12 to 12
- arrival: int32 [32], replicated, may hold values from 0 to 31, each once
- bucket_of_row: int32 [32], replicated, may hold values from 0 to 15, never falling along the last dimension, each value on 1 to 4 neighbouring positions
Outputs:
- unit_codes: bfloat16 [4, 32, 18432], P(None, 'dp', 'tensor')
- bucket_peaks: float32 [4, 16], replicated
- compensated: float32 [32, 18432], P('dp', 'tensor')
Inputs may be any that keep to these rules, and one draw needn't show every extreme that they name: `arrival`: each weight row appears in exactly one slot. `bucket_of_row`: bucket numbers never fall along the rows; each bucket holds 1 to 4 consecutive rows and one holds exactly 4.
All inputs are finite; a program needn't handle non-finite values.
Results may differ from a plain program's by a relative error of at most 0.001.
Values sent between devices are 32-bit elements; how exact they have to be, the bound alone decides.
A program may use at most 64 MiB of HBM per device.

v0:
```python
import jax
import jax.numpy as jnp
from jax import lax
from jax.sharding import PartitionSpec as P

NB = 16


epsilon = 1e-06


def on_device(grad_codes, exponents, accumulated, arrival, bucket_of_row):
    row_count = arrival.shape[0]
    own_rows = accumulated.shape[0]
    step_count = grad_codes.shape[0]
    inverse = (
        jnp.zeros((row_count,), jnp.int32).at[arrival].set(jnp.arange(row_count, dtype=jnp.int32))
    )
    member = bucket_of_row[:, None] == jnp.arange(NB, dtype=jnp.int32)[None, :]
    factors = jnp.exp2(-exponents[:, 0, :].astype(jnp.float32))
    reduced = []
    for micro_step in range(step_count):
        row_block = jnp.take(grad_codes[micro_step, 0], inverse, axis=0)
        factor_rows = jnp.sum(jnp.where(member, factors[micro_step][None, :], 0.0), axis=1)
        reduced.append(
            lax.psum_scatter(
                row_block.astype(jnp.float32) * factor_rows[:, None],
                "dp",
                scatter_dimension=0,
                tiled=True,
            )
        )
    own_member = lax.dynamic_slice_in_dim(member, lax.axis_index("dp") * own_rows, own_rows, 0)
    running = accumulated
    carried = jnp.zeros(accumulated.shape, jnp.float32)
    exact_sums = []
    local_peaks = []
    for micro_step in range(step_count):
        adjusted = reduced[micro_step] - carried
        previous = running.astype(jnp.float32)
        running = lax.optimization_barrier((previous + adjusted).astype(jnp.bfloat16))
        carried = running.astype(jnp.float32) - previous - adjusted
        exact_sum = running.astype(jnp.float32) - carried
        exact_sums.append(exact_sum)
        row_max = jnp.max(jnp.abs(exact_sum), axis=1)
        local_peak = jnp.max(jnp.where(own_member, row_max[:, None], 0.0), axis=0)
        local_peaks.append(local_peak)
    peak_table = lax.pmax(jnp.stack(local_peaks), ("dp", "tensor"))
    scaled_list = []
    for micro_step in range(step_count):
        peak_rows = jnp.sum(jnp.where(own_member, peak_table[micro_step][None, :], 0.0), axis=1)
        scaled_list.append(
            (exact_sums[micro_step] / (peak_rows[:, None] + epsilon)).astype(jnp.bfloat16)
        )
    return (jnp.stack(scaled_list), peak_table, exact_sums[-1])


def solution(mesh):
    return jax.shard_map(
        on_device,
        mesh=mesh,
        in_specs=(P(None, "dp", None, "tensor"), P(None, "dp", None), P("dp", "tensor"), P(), P()),
        out_specs=(P(None, "dp", "tensor"), P(), P("dp", "tensor")),
        check_vma=False,
    )
```

profile of v0, /device:TPU:0, one launch (start us, length us, event | category | flops | bytes accessed | tf_op | source)
XLA Modules:
  0.0 292.9 jit_solution(1497230470534958042)
XLA Ops:
  7.2 0.0 all-reduce.7.cloned.1.call-start
  7.2 0.7 compare_select_fusion.1
  7.9 0.7 scatter_custom_fusion
  8.6 0.5 compare_and_fusion
  9.1 0.7 multiply_exponential_fusion
  9.8 0.5 slice_bitcast_fusion.7
  10.3 3.8 %slice_bitcast_fusion = (bf16[32,18432]{1,0:T(8,128)(2,1)S(1)}, bf16[32,18432]{1,0:T(8,128)(2,1)S(1)}, bf16[32,18432]{1,0:T(8,128)(2,1)}, bf16[32,18432]{1,0:T(8,128)(2,1)S(1)}) fusion(bf16[4,1,32,18432]{3,2,1,0:T(8,128)(2,1)} %param.7), kind=kLoop, calls=%fused_computation.9 | loop fusion | bytes 9437184 | tf_op jit(solution)/shard_map/squeeze | solution.py:23
  14.1 4.8 %gather_fusion = bf16[32,18432]{1,0:T(8,128)(2,1)} fusion(bf16[32,18432]{1,0:T(8,128)(2,1)} %get-tuple-element.28, s32[1024]{0:T(1024)S(1)} %pad_clamp_fusion), kind=kCustom, calls=%fused_computation.clone | custom fusion | bytes 2359424 | tf_op jit(solution)/shard_map/jit(_take)/gather | solution.py:23
  18.8 2.3 gather_fusion.1
  21.1 2.3 gather_fusion.2
  23.5 0.0 copy-start.5
  23.5 0.0 copy-start
  23.5 0.0 copy-start.1
  23.5 2.3 gather_fusion.3
  25.8 0.0 copy-done.5
  25.8 0.9 select_reduce_fusion
  26.7 0.0 copy-done
  26.7 0.0 copy-done.1
  26.7 5.7 %convert_multiply_fusion = (f32[32,18432]{1,0:T(8,128)}, f32[32,18432]{1,0:T(8,128)}, f32[32,18432]{1,0:T(8,128)}, f32[32,18432]{1,0:T(8,128)}) fusion(bf16[32,18432]{1,0:T(8,128)(2,1)} %gather_fusion.3, f32[32]{0:T(128)S(1)} %get-tuple-element.8, pred[32]{0:T(512)(128)(4,1)} %compare_and_fusion, f32[32]{0:T(128)S(1)} %get-tuple-element.10, ...), kind=kLoop, calls=%fused_computation.5 | loop fusion | flops 7077888 | bytes 14156320 | tf_op jit(solution)/shard_map/mul | solution.py:27
  32.4 0.0 copy-start.2
  32.4 0.0 all-reduce.7.cloned.1.call-update
  32.4 0.1 iota_compare_fusion
  32.5 193.9 %all-reduce.7.cloned.1.call-done = (f32[32,18432]{1,0:T(8,128)}, f32[32,18432]{1,0:T(8,128)}, f32[32,18432]{1,0:T(8,128)}, f32[32,18432]{1,0:T(8,128)}) async-done(((f32[32,18432]{1,0:T(8,128)}, f32[32,18432]{1,0:T(8,128)}, f32[32,18432]{1,0:T(8,128)}, f32[32,18432]{1,0:T(8,128)}), (f32[32,18432]{1,0:T(8,128)}, f32[32,18432]{1,0:T(8,128)}, f32[32,18432]{1,0:T(8,128)}, ...) | async-done | bytes 9437200
  226.4 0.0 copy-done.2
  226.4 1.2 add_convert_fusion.3
  227.6 1.9 abs_reduce_fusion.3
  229.5 1.2 add_convert_fusion.2
  230.6 1.9 abs_reduce_fusion.2
  232.5 1.2 add_convert_fusion.1
  233.7 1.9 abs_reduce_fusion.1
  235.6 1.2 add_convert_fusion
  236.8 1.9 abs_reduce_fusion
  238.7 0.0 copy-start.3
  238.7 0.7 broadcast_select_fusion.3
  239.4 1.8 broadcast_select_fusion.2
  241.2 40.3 %pmax.7 = f32[4,16]{1,0:T(4,128)S(1)} all-reduce(f32[4,16]{1,0:T(4,128)S(1)} %pad_maximum_fusion.1), channel_id=1, replica_groups=mesh['dp'=32,'tensor'=1] {'dp','tensor'}, use_global_device_ids=true, to_apply=%region_13.15 | all-reduce | flops 64 | bytes 512 | tf_op jit(solution)/shard_map/pmax | solution.py:48
  281.5 0.0 copy-start.4
  281.5 0.7 select_reduce_fusion.7
  284.7 0.2 convert_bitcast_fusion.2
  284.9 0.2 convert_bitcast_fusion
  285.1 1.0 pad_maximum_fusion
  286.1 0.0 copy-done.3
  286.1 0.0 copy-done.4
  (4 shorter events, 0.0 us)
Async XLA Ops:
  7.2 219.3 %all-reduce.7.cloned.1.call-start = ((), (), s32[]{:S(2)}) async-start(), calls=%async_computation | async-start | bytes 18874368
  23.5 2.3 copy-start.5
  23.5 3.2 %copy-start = (bf16[32,18432]{1,0:T(8,128)(2,1)S(1)}, bf16[32,18432]{1,0:T(8,128)(2,1)}, u32[]{:S(2)}) copy-start(bf16[32,18432]{1,0:T(8,128)(2,1)} %gather_fusion) | copy-start | bytes 3538948
  23.5 3.2 %copy-start.1 = (bf16[32,18432]{1,0:T(8,128)(2,1)S(1)}, bf16[32,18432]{1,0:T(8,128)(2,1)}, u32[]{:S(2)}) copy-start(bf16[32,18432]{1,0:T(8,128)(2,1)} %gather_fusion.1) | copy-start | bytes 3538948
  32.4 194.0 %copy-start.2 = (bf16[1,18432]{1,0:T(2,128)(2,1)S(1)}, bf16[1,18432]{1,0:T(2,128)(2,1)}, u32[]{:S(2)}) copy-start(bf16[1,18432]{1,0:T(2,128)(2,1)} %param.9) | copy-start | bytes 110596
  238.7 47.4 %copy-start.3 = (f32[1,18432]{1,0:T(1,128)}, f32[1,18432]{1,0:T(1,128)S(1)}, u32[]{:S(2)}) copy-start(f32[1,18432]{1,0:T(1,128)S(1)} %get-tuple-element.25) | copy-start | bytes 221188
  281.5 4.6 %copy-start.4 = (f32[4,16]{1,0:T(4,128)}, f32[4,16]{1,0:T(4,128)S(1)}, u32[]{:S(2)}) copy-start(f32[4,16]{1,0:T(4,128)S(1)} %pmax.7) | copy-start | bytes 772
Sparse Core Ops, SparseCore 0:
  32.5 193.8 all-reduce.6
where the time goes:
time: 294 us; the launch traced here: 293 us
  waiting for transfers between devices  194 us (66%)
  blocking collectives  40.3 us (14%)
  other arithmetic  25.4 us (9%)
  local copies, waits for them, and re-layouts  16.7 us (6%)
  between operations  16.7 us (6%)
    unnamed x2, waiting for transfers between devices  194 us
    pmax x1, blocking collectives, on_device(): peak_table = lax.pmax(jnp.stack(local_peaks), ('dp', 'tensor'))  40.3 us
    gather x4, local copies, waits for them, and re-layouts, on_device(): row_block = jnp.take(grad_codes[micro_step, 0], inverse, axis=0)  11.7 us
    reduce_max x4, other arithmetic, on_device(): row_max = jnp.max(jnp.abs(exact_sum), axis=1)  7.55 us
  transfers between devices with their start and end apart: 1, of which 1 were waited for; matrix products, arithmetic and copies ran while one was open for 0% of the time, Pallas kernels for 0%

commit v1 on v0

v1 whole, which is shorter than its diff:
```python
import functools

import jax
import jax.numpy as jnp
from jax import lax
from jax.experimental import pallas as pl
from jax.experimental.pallas import tpu as pltpu
from jax.sharding import PartitionSpec as P

epsilon = 1e-06
LANES = 128


def bit_orders(bits):
    head = list(range(1, min(4, bits)))
    tail = list(range(1 + len(head), bits))
    return [[0] + head[r:] + head[:r] + tail for r in range(max(1, len(head)))]


def widths_of(tiles, count):
    if count == 1:
        return [tiles]
    first = -(-tiles * 8 // 18)
    last = tiles * 4 // 18
    return [first, tiles - first - last, last]


def exchange(n, steps, rows, groups, orders, spans, codes, meta, start, exact, table, x, lhs, out, acc, r0, r1, peak,
             x_sem, send_sem, recv_sem, peak_send, peak_recv):
    me = lax.axis_index("dp")
    bits = n.bit_length() - 1
    half = rows // 2
    width = x.shape[2]
    lands = [r0] + list(r1)
    loads = []
    for s in range(steps):
        for g in range(groups):
            copy = pltpu.make_async_copy(
                codes.at[s, 0, :, pl.ds(g * width, width)], x.at[s, pl.ds(g * rows, rows), :], x_sem.at[s, g]
            )
            copy.start()
            loads.append(copy)

    barrier = pltpu.get_barrier_semaphore()

    def greet(j, carry):
        pl.semaphore_signal(barrier, inc=1, device_id={"dp": lax.rem(me + j, n)}, device_id_type=pl.DeviceIdType.MESH)
        return carry

    lax.fori_loop(1, n, greet, 0)

    partners = []
    for b in range(bits):
        stride = 1 << b
        bit = lax.rem(me // stride, 2)
        partners.append(me + stride * (1 - 2 * bit))

    size = groups * rows
    row_id = lax.broadcasted_iota(jnp.int32, (size, size), 0)
    col_id = lax.broadcasted_iota(jnp.int32, (size, size), 1)
    same_group = (row_id % groups) == (col_id // rows)
    position = row_id // groups
    masks = []
    for order in orders:
        owner = jnp.zeros_like(position)
        for m, b in enumerate(order):
            bit = (position // (1 << (bits - 1 - m))) % 2
            mine = lax.rem(me // (1 << b), 2)
            owner = owner + ((bit + mine) % 2) * (1 << b)
        masks.append(same_group & (owner.astype(jnp.float32) == meta[steps : steps + 1, :]))
    for q in range(len(orders)):
        for s in range(steps):
            lhs[q, s] = jnp.where(masks[q], meta[s : s + 1, :], 0.0).astype(jnp.bfloat16)

    def copy_of(s, q, k):
        at, wide = spans[q]
        count = half >> k
        source = out.at[s, :, :, pl.ds(at, wide)] if k == 0 else acc.at[s, pl.ds(count, count), :, pl.ds(at, wide)]
        return pltpu.make_async_remote_copy(
            src_ref=source,
            dst_ref=lands[k].at[s, :, :, pl.ds(at, wide)],
            send_sem=send_sem.at[s, q, k],
            recv_sem=recv_sem.at[s, q, k],
            device_id={"dp": partners[orders[q][k]]},
            device_id_type=pl.DeviceIdType.MESH,
        )

    def stage(s, q, k):
        at, wide = spans[q]
        cols = pl.ds(at, wide)
        if k == 0:
            split = half * groups
            part = jnp.dot(lhs[q, s, split:, :], x[s, :, cols], preferred_element_type=jnp.float32)
            out[s, :, :, cols] = part.reshape(half, groups, wide)
            if s == 0 and q == 0:
                pl.semaphore_wait(barrier, n - 1)
            copy_of(s, q, 0).start()
            part = jnp.dot(lhs[q, s, :split, :], x[s, :, cols], preferred_element_type=jnp.float32)
            acc[s, :, :, cols] = part.reshape(half, groups, wide)
            return
        copy_of(s, q, k - 1).wait_recv()
        count = half >> k
        got = lands[k - 1]
        if k < bits:
            acc[s, count : 2 * count, :, cols] += got[s, count : 2 * count, :, cols]
            copy_of(s, q, k).start()
            acc[s, 0:count, :, cols] += got[s, 0:count, :, cols]
        else:
            acc[s, 0:1, :, cols] += got[s, 0:1, :, cols]

    state = [start[...], jnp.zeros_like(start)]
    peaks = []
    for wave in range(steps + bits):
        for k in range(bits + 1):
            s = wave - k
            if s < 0 or s >= steps:
                continue
            if k == 0:
                for copy in loads[s * groups : (s + 1) * groups]:
                    copy.wait()
            for q in range(len(orders)):
                stage(s, q, k)
            if k == bits:
                running, carried = state
                adjusted = acc[s, 0] - carried
                new = (running + adjusted).astype(jnp.bfloat16).astype(jnp.float32)
                carried = (new - running) - adjusted
                state = [new, carried]
                total = new - carried
                exact[s] = total
                peaks.append(jnp.max(jnp.max(jnp.abs(total), axis=0, keepdims=True), axis=1, keepdims=True))

    lane = lax.broadcasted_iota(jnp.int32, (1, LANES), 1)
    row = jnp.zeros((1, LANES), jnp.float32)
    for s in range(steps):
        row = jnp.where(lane == s, peaks[s], row)
    peak[...] = row

    def peak_copy(j):
        return pltpu.make_async_remote_copy(
            src_ref=peak,
            dst_ref=table.at[me],
            send_sem=peak_send.at[j],
            recv_sem=peak_recv.at[j],
            device_id={"dp": lax.rem(me + j, n)},
            device_id_type=pl.DeviceIdType.MESH,
        )

    def tell(j, carry):
        peak_copy(j).start()
        return carry

    def hear(j, carry):
        peak_copy(j).wait()
        return carry

    lax.fori_loop(1, n, tell, 0)
    table[me] = row
    for s in range(steps):
        for q in range(len(orders)):
            for k in range(bits):
                copy_of(s, q, k).wait_send()
    lax.fori_loop(1, n, hear, 0)


def on_device(n, tensor, grad_codes, exponents, accumulated, arrival, bucket_of_row):
    steps, _, rows, columns = grad_codes.shape
    buckets = exponents.shape[2]
    bits = n.bit_length() - 1
    groups = max(g for g in (1, 2, 4, 8) if columns % (g * LANES) == 0)
    width = columns // groups
    orders = bit_orders(bits)
    spans, at = [], 0
    for tiles in widths_of(width // LANES, len(orders)):
        spans.append((at, tiles * LANES))
        at += tiles * LANES

    member = bucket_of_row[:, None] == jnp.arange(buckets, dtype=jnp.int32)[None, :]
    factors = jnp.exp2(-exponents[:, 0, :].astype(jnp.float32))
    factor_rows = jnp.sum(jnp.where(member[None], factors[:, None, :], 0.0), axis=2)
    holds = arrival[:, None] == jnp.arange(rows, dtype=jnp.int32)[None, :]
    factor_slots = jnp.sum(jnp.where(holds[None], factor_rows[:, None, :], 0.0), axis=2)
    meta = jnp.tile(jnp.concatenate([factor_slots, arrival[None].astype(jnp.float32)]), (1, groups))

    half = rows // 2
    vmem = pl.BlockSpec(memory_space=pltpu.VMEM)
    exact, table = pl.pallas_call(
        functools.partial(_entry, n, steps, rows, groups, orders, spans, bits),
        out_shape=(
            jax.ShapeDtypeStruct((steps, groups, width), jnp.float32),
            jax.ShapeDtypeStruct((n, 1, LANES), jnp.float32),
        ),
        in_specs=[pl.BlockSpec(memory_space=pl.ANY), vmem, vmem],
        out_specs=(vmem, vmem),
        scratch_shapes=[
            pltpu.VMEM((steps, groups * rows, width), jnp.bfloat16),
            pltpu.VMEM((len(orders), steps, groups * rows, groups * rows), jnp.bfloat16),
            pltpu.VMEM((steps, half, groups, width), jnp.float32),
            pltpu.VMEM((steps, half, groups, width), jnp.float32),
        ]
        + [pltpu.VMEM((steps, half >> k, groups, width), jnp.float32) for k in range(bits)]
        + [
            pltpu.VMEM((1, LANES), jnp.float32),
            pltpu.SemaphoreType.DMA((steps, groups)),
            pltpu.SemaphoreType.DMA((steps, len(orders), bits)),
            pltpu.SemaphoreType.DMA((steps, len(orders), bits)),
            pltpu.SemaphoreType.DMA((n,)),
            pltpu.SemaphoreType.DMA((n,)),
        ],
        compiler_params=pltpu.CompilerParams(
            collective_id=0, has_side_effects=True, vmem_limit_bytes=56 * 1024 * 1024
        ),
    )(grad_codes, meta, accumulated.astype(jnp.float32).reshape(groups, width))

    row_peaks = table[:, 0, :steps]
    peak_table = jnp.max(jnp.where(member[:, None, :], row_peaks[:, :, None], 0.0), axis=0)
    if tensor > 1:
        peak_table = lax.pmax(peak_table, "tensor")
    own = lax.dynamic_slice_in_dim(member, lax.axis_index("dp"), 1, 0)
    own_peaks = jnp.sum(jnp.where(own, peak_table, 0.0), axis=1)
    unit = (exact / (own_peaks[:, None, None] + epsilon)).astype(jnp.bfloat16)
    return unit.reshape(steps, 1, columns), peak_table, exact[-1].reshape(1, columns)


def _entry(n, steps, rows, groups, orders, spans, bits, codes, meta, start, exact, table, x, lhs, out, acc, *rest):
    lands, others = rest[:bits], rest[bits:]
    exchange(n, steps, rows, groups, orders, spans, codes, meta, start, exact, table, x, lhs, out, acc,
             lands[0], lands[1:], *others)


def solution(mesh):
    return jax.shard_map(
        functools.partial(on_device, mesh.shape["dp"], mesh.shape["tensor"]),
        mesh=mesh,
        in_specs=(P(None, "dp", None, "tensor"), P(None, "dp", None), P("dp", "tensor"), P(), P()),
        out_specs=(P(None, "dp", "tensor"), P(), P("dp", "tensor")),
        check_vma=False,
    )
```

time: 294 us -> 69.3 us (0.24)
  waiting for transfers between devices: 194 us -> 0 us
  Pallas kernels: 0 us -> 58.3 us
  blocking collectives: 40.3 us -> 0 us
  other arithmetic: 25.4 us -> 5.29 us
  between operations: 16.7 us -> 0.69 us
  local copies, waits for them, and re-layouts: 16.7 us -> 4.66 us
    unnamed x2 -> x0, waiting for transfers between devices: 194 us -> none
    pallas_call x0 -> x1, Pallas kernels: none -> 58.3 us  [on_device(): pl.pallas_call(functools.partial(_entry, n, steps, rows, groups, orders,...]
    pmax x1 -> x0, blocking collectives: 40.3 us -> none  [on_device(): peak_table = lax.pmax(jnp.stack(local_peaks), ('dp', 'tensor'))]
    gather x4 -> x0, local copies, waits for them, and re-layouts: 11.7 us -> none  [on_device(): row_block = jnp.take(grad_codes[micro_step, 0], inverse, axis=0)]
    reduce_max x4 -> x1, other arithmetic: 7.55 us -> 0.09 us  [on_device(): jnp.max(jnp.where(member[:, None, :], row_peaks[:, :, None], 0.0), axis=0)]
    mul x1 -> x0, other arithmetic: 5.71 us -> none  [on_device(): row_block.astype(jnp.float32) * factor_rows[:, None]]
    squeeze x1 -> x0, local copies, waits for them, and re-layouts: 3.76 us -> none  [on_device(): row_block = jnp.take(grad_codes[micro_step, 0], inverse, axis=0)]
    select_n x4 -> x0, other arithmetic: 3.15 us -> none  [the longest x2 2.49 us: on_device(): local_peak = jnp.max(jnp.where(own_member, row_max[:, None], 0.0), axis=0)]
  transfers between devices with their start and end apart: 1 -> 0, of which waited for: 1 -> 0; matrix products, arithmetic and copies ran while one was open for 0% -> 0% of each run, Pallas kernels for 0% -> 0%
where the time goes in v1:
time: 69.3 us; the launch traced here: 68.9 us
  Pallas kernels  58.3 us (84%)
  other arithmetic  5.29 us (8%)
  local copies, waits for them, and re-layouts  4.66 us (7%)
    pallas_call x1, Pallas kernels, on_device(): pl.pallas_call(functools.partial(_entry, n, steps, rows, groups, orders,...  58.3 us
    unnamed x4, local copies, waits for them, and re-layouts  1.61 us

profile of v1, /device:TPU:0, one launch (start us, length us, event | category | flops | bytes accessed | tf_op | source)
XLA Modules:
  0.0 68.9 jit_solution(5679269130204863041)
XLA Ops:
  0.6 0.7 convert_bitcast_fusion
  1.3 0.7 iota_compare_fusion.1
  2.0 0.2 dynamic-slice_reduce_fusion
  2.1 0.7 %multiply_exponential_fusion = f32[4,1,16]{2,1,0:T(1,128)S(1)} fusion(s32[4,1,16]{2,1,0:T(1,128)} %param.6), kind=kLoop, calls=%fused_computation.11 | loop fusion | flops 192 | bytes 512 | tf_op jit(solution)/shard_map/exp2 | solution.py:179
  2.8 0.1 select_reduce_fusion.2
  2.9 0.7 %iota_compare_fusion = pred[32,32]{1,0:T(8,128)(4,1)S(1)} fusion(s32[32]{0:T(128)} %param.8), kind=kLoop, calls=%fused_computation.6 | loop fusion | flops 1024 | bytes 1152 | tf_op jit(solution)/shard_map/eq | solution.py:181
  3.7 0.1 select_reduce_fusion
  3.8 0.7 tile.10.meta
  4.5 1.1 %convert_reduce_fusion = f32[18432]{0:T(1024)S(1)} fusion(bf16[1,18432]{1,0:T(2,128)(2,1)} %param.7), kind=kLoop, calls=%fused_computation.1 | loop fusion | flops 18432 | bytes 110592 | tf_op jit(solution)/shard_map/reshape | solution.py:213
  5.6 0.6 reshape.80.start
  6.2 58.3 %shard_map.76 = (f32[4,8,2304]{2,1,0:T(8,128)}, f32[32,1,128]{2,1,0:T(1,128)}) custom-call(bf16[4,1,32,18432]{3,2,1,0:T(8,128)(2,1)} %codes.1, f32[5,256]{1,0:T(8,128)} %tile.10.meta, f32[8,2304]{1,0:T(8,128)} %reshape.80.start), custom_call_target="tpu_custom_call" | custom-call | tf_op jit(solution)/shard_map/pallas_call | solution.py:187
  64.5 0.8 %copy.14 = f32[32,1,4]{0,2,1:T(4,128)S(1)} copy(f32[32,1,4]{2,1,0:T(1,128)} %bitcast.9) | data formatting | bytes 1024 | tf_op jit(solution)/shard_map/slice | solution.py:215
  65.3 0.1 select_reduce_fusion.1
  65.4 0.0 copy-start
  65.4 0.1 select_reduce_fusion.3
  65.5 0.9 %slice_bitcast_fusion = f32[1,1,8,2304]{3,2,1,0:T(8,128)S(1)} fusion(f32[4,8,2304]{2,1,0:T(8,128)} %get-tuple-element.5), kind=kLoop, calls=%fused_computation.2 | loop fusion | bytes 147456
  66.4 1.1 %divide_convert_fusion = bf16[4,8,2304]{2,1,0:T(8,128)(2,1)S(1)} fusion(f32[4,8,2304]{2,1,0:T(8,128)} %get-tuple-element.5, f32[4]{0:T(128)S(1)} %broadcast_add_fusion), kind=kLoop, calls=%fused_computation | loop fusion | flops 147456 | bytes 442384 | tf_op jit(solution)/shard_map/convert_element_type | solution.py:221
  67.5 0.7 %reshape.78 = bf16[4,1,18432]{2,0,1:T(4,128)(2,1)} reshape(bf16[4,8,2304]{2,1,0:T(8,128)(2,1)S(1)} %divide_convert_fusion) | data formatting | bytes 294912 | tf_op jit(solution)/shard_map/reshape | solution.py:222
  68.2 0.7 %copy.15 = f32[1,1,8,2304]{3,1,2,0:T(1,128)} copy(f32[1,1,8,2304]{3,2,1,0:T(8,128)S(1)} %slice_bitcast_fusion) | data formatting | bytes 147456
  68.9 0.0 copy-done
  (3 shorter events, 0.0 us)
Async XLA Ops:
  65.4 3.5 %copy-start = (f32[4,16]{1,0:T(4,128)}, f32[4,16]{1,0:T(4,128)S(1)}, u32[]{:S(2)}) copy-start(f32[4,16]{1,0:T(4,128)S(1)} %select_reduce_fusion.1) | copy-start | bytes 772

commit v2 on v1

v2 whole, which is shorter than its diff:
```python
import functools

import jax
import jax.numpy as jnp
from jax import lax
from jax.experimental import pallas as pl
from jax.experimental.pallas import tpu as pltpu
from jax.sharding import PartitionSpec as P

epsilon = 1e-06
LANES = 128


def bit_orders(bits):
    head = list(range(1, min(4, bits)))
    tail = list(range(1 + len(head), bits))
    return [[0] + head[r:] + head[:r] + tail for r in range(max(1, len(head)))]


def chunks_of(tiles, count):
    plans = {18: PLAN}
    plan = plans.get(tiles, [(1,) * count] * (tiles // count)) if count == 3 else [(tiles,) + (0,) * (count - 1)]
    plan = [list(row) for row in plan]
    plan[0][0] += tiles - sum(map(sum, plan))
    spans, at = [], 0
    for row in plan:
        spans.append([])
        for wide in row:
            spans[-1].append((at * LANES, wide * LANES))
            at += wide
    return spans


PLAN = [(2, 1, 1), (2, 2, 1), (2, 2, 1), (2, 1, 1)]


def exchange(n, orders, spans, codes, exponents, accumulated, arrival, bucket_of_row, exact, peak_table, own_peak, x, lhs,
             begin, out, acc, peak, table, x_sem, send_sem, recv_sem, peak_send, peak_recv, *lands):
    me = lax.axis_index("dp")
    bits = n.bit_length() - 1
    steps, size, width = x.shape
    rows = codes.shape[2]
    groups = size // rows
    half = rows // 2
    loads = []
    for c, row in enumerate(spans):
        first, wide = row[0][0], sum(w for _, w in row)
        loads.append([])
        for g in range(groups):
            copy = pltpu.make_async_copy(
                codes.at[:, 0, :, pl.ds(g * width + first, wide)],
                x.at[:, pl.ds(g * rows, rows), pl.ds(first, wide)],
                x_sem.at[c, g],
            )
            copy.start()
            loads[-1].append(copy)

    barrier = pltpu.get_barrier_semaphore()

    def greet(j, carry):
        pl.semaphore_signal(barrier, inc=1, device_id={"dp": lax.rem(me + j, n)}, device_id_type=pl.DeviceIdType.MESH)
        return carry

    lax.fori_loop(1, n, greet, 0)

    partners = []
    for b in range(bits):
        stride = 1 << b
        bit = lax.rem(me // stride, 2)
        partners.append(me + stride * (1 - 2 * bit))

    slot = lax.broadcasted_iota(jnp.int32, (1, size), 1) % rows
    held = jnp.zeros((1, size), jnp.int32)
    scale = [jnp.zeros((1, size), jnp.int32) for _ in range(steps)]
    for k in range(rows):
        row = arrival[k]
        bucket = bucket_of_row[row]
        here = slot == k
        held = jnp.where(here, row, held)
        for s in range(steps):
            scale[s] = jnp.where(here, exponents[s, 0, bucket], scale[s])
    scale = [jnp.exp2(-e.astype(jnp.float32)) for e in scale]

    row_group = lax.broadcasted_iota(jnp.int32, (size, 1), 0) % groups
    col_group = lax.broadcasted_iota(jnp.int32, (1, size), 1) // rows
    wanted = held * groups + col_group
    place = lax.broadcasted_iota(jnp.int32, (size, 1), 0) // groups
    for q, order in enumerate(orders):
        owner = jnp.zeros_like(place)
        for m, b in enumerate(order):
            bit = (place // (1 << (bits - 1 - m))) % 2
            mine = lax.rem(me // (1 << b), 2)
            owner = owner + ((bit + mine) % 2) * (1 << b)
        mask = owner * groups + row_group == wanted
        for s in range(steps):
            lhs[q, s] = jnp.where(mask, scale[s], 0.0).astype(jnp.bfloat16)
    for g in range(groups):
        begin[g : g + 1, :] = accumulated[:, g * width : (g + 1) * width].astype(jnp.float32)

    def copy_of(c, q, k):
        at, wide = spans[c][q]
        count = half >> k
        cols = pl.ds(at, wide)
        source = out.at[:, :, :, cols] if k == 0 else acc.at[:, pl.ds(count, count), :, cols]
        return pltpu.make_async_remote_copy(
            src_ref=source,
            dst_ref=lands[k].at[:, :, :, cols],
            send_sem=send_sem.at[c, q, k],
            recv_sem=recv_sem.at[c, q, k],
            device_id={"dp": partners[orders[q][k]]},
            device_id_type=pl.DeviceIdType.MESH,
        )

    def stage(c, q, k):
        at, wide = spans[c][q]
        cols = pl.ds(at, wide)
        if k == 0:
            split = half * groups
            for s in range(steps):
                part = jnp.dot(lhs[q, s], x[s, :, cols], preferred_element_type=jnp.float32)
                out[s, :, :, cols] = part[split:].reshape(half, groups, wide)
                acc[s, :, :, cols] = part[:split].reshape(half, groups, wide)
            if c == 0 and q == 0:
                pl.semaphore_wait(barrier, n - 1)
            copy_of(c, q, 0).start()
            return
        copy_of(c, q, k - 1).wait_recv()
        count = half >> k
        got = lands[k - 1]
        if k < bits:
            acc[:, count : 2 * count, :, cols] += got[:, count : 2 * count, :, cols]
            copy_of(c, q, k).start()
            acc[:, 0:count, :, cols] += got[:, 0:count, :, cols]
        else:
            acc[:, 0:1, :, cols] += got[:, 0:1, :, cols]

    tops = [jnp.zeros((groups, 1), jnp.float32) for _ in range(steps)]
    for wave in range(len(spans) + bits):
        for k in range(bits + 1):
            c = wave - k
            if c < 0 or c >= len(spans):
                continue
            streams = [q for q in range(len(orders)) if spans[c][q][1]]
            if k == 0:
                for copy in loads[c]:
                    copy.wait()
            for q in streams:
                stage(c, q, k)
            if k == bits:
                first, wide = spans[c][0][0], sum(w for _, w in spans[c])
                running = begin[:, first : first + wide]
                carried = jnp.zeros_like(running)
                for s in range(steps):
                    adjusted = acc[s, 0, :, first : first + wide] - carried
                    new = (running + adjusted).astype(jnp.bfloat16).astype(jnp.float32)
                    carried = (new - running) - adjusted
                    running = new
                    total = new - carried
                    tops[s] = jnp.maximum(tops[s], jnp.max(jnp.abs(total), axis=1, keepdims=True))
                    for g in range(groups):
                        exact[s : s + 1, g * width + first : g * width + first + wide] = total[g : g + 1, :]

    lane = lax.broadcasted_iota(jnp.int32, (1, LANES), 1)
    row = jnp.zeros((1, LANES), jnp.float32)
    for s in range(steps):
        row = jnp.where(lane == s, jnp.max(tops[s], axis=0, keepdims=True), row)
    peak[...] = row

    def peak_copy(j):
        return pltpu.make_async_remote_copy(
            src_ref=peak,
            dst_ref=table.at[me],
            send_sem=peak_send.at[j],
            recv_sem=peak_recv.at[j],
            device_id={"dp": lax.rem(me + j, n)},
            device_id_type=pl.DeviceIdType.MESH,
        )

    def tell(j, carry):
        peak_copy(j).start()
        return carry

    def hear(j, carry):
        peak_copy(j).wait()
        return carry

    lax.fori_loop(1, n, tell, 0)
    table[me] = row
    for c in range(len(spans)):
        for q in range(len(orders)):
            if spans[c][q][1]:
                for k in range(bits):
                    copy_of(c, q, k).wait_send()
    lax.fori_loop(1, n, hear, 0)

    buckets = exponents.shape[2]
    by_bucket = jnp.zeros((buckets, LANES), jnp.float32)
    own = jnp.zeros((1, LANES), jnp.float32)
    bucket_id = lax.broadcasted_iota(jnp.int32, (buckets, LANES), 0)
    lane_id = lax.broadcasted_iota(jnp.int32, (buckets, LANES), 1)
    my_bucket = bucket_of_row[me]
    for i in range(rows):
        bucket = bucket_of_row[i]
        by_bucket = jnp.maximum(by_bucket, jnp.where(bucket_id == bucket, table[i], 0.0))
    own = jnp.max(jnp.where(bucket_id == my_bucket, by_bucket, 0.0), axis=0, keepdims=True)
    for s in range(steps):
        turned = jnp.sum(jnp.where(bucket_id == lane_id, by_bucket[:, s : s + 1], 0.0), axis=0, keepdims=True)
        peak_table[s : s + 1, :] = turned[:, :buckets]
        own_peak[s : s + 1, :] = jnp.broadcast_to(own[:, s : s + 1], (1, LANES))


def on_device(n, tensor, grad_codes, exponents, accumulated, arrival, bucket_of_row):
    steps, _, rows, columns = grad_codes.shape
    buckets = exponents.shape[2]
    bits = n.bit_length() - 1
    groups = max(g for g in (1, 2, 4, 8) if columns % (g * LANES) == 0)
    width = columns // groups
    orders = bit_orders(bits)
    spans = chunks_of(width // LANES, len(orders))
    half = rows // 2
    vmem = pl.BlockSpec(memory_space=pltpu.VMEM)
    smem = pl.BlockSpec(memory_space=pltpu.SMEM)
    exact, peak_table, own_peaks = pl.pallas_call(
        functools.partial(exchange, n, orders, spans),
        out_shape=(
            jax.ShapeDtypeStruct((steps, columns), jnp.float32),
            jax.ShapeDtypeStruct((steps, buckets), jnp.float32),
            jax.ShapeDtypeStruct((steps, LANES), jnp.float32),
        ),
        in_specs=[pl.BlockSpec(memory_space=pl.ANY), smem, vmem, smem, smem],
        out_specs=(vmem, vmem, vmem),
        scratch_shapes=[
            pltpu.VMEM((steps, groups * rows, width), jnp.bfloat16),
            pltpu.VMEM((len(orders), steps, groups * rows, groups * rows), jnp.bfloat16),
            pltpu.VMEM((groups, width), jnp.float32),
            pltpu.VMEM((steps, half, groups, width), jnp.float32),
            pltpu.VMEM((steps, half, groups, width), jnp.float32),
            pltpu.VMEM((1, LANES), jnp.float32),
            pltpu.VMEM((n, 1, LANES), jnp.float32),
            pltpu.SemaphoreType.DMA((len(spans), groups)),
            pltpu.SemaphoreType.DMA((len(spans), len(orders), bits)),
            pltpu.SemaphoreType.DMA((len(spans), len(orders), bits)),
            pltpu.SemaphoreType.DMA((n,)),
            pltpu.SemaphoreType.DMA((n,)),
        ]
        + [pltpu.VMEM((steps, half >> k, groups, width), jnp.float32) for k in range(bits)],
        compiler_params=pltpu.CompilerParams(
            collective_id=0, has_side_effects=True, vmem_limit_bytes=56 * 1024 * 1024
        ),
    )(grad_codes, exponents, accumulated, arrival, bucket_of_row)

    own_peaks = own_peaks[:, :1]
    if tensor > 1:
        peak_table = lax.pmax(peak_table, "tensor")
        own = lax.dynamic_slice_in_dim(bucket_of_row, lax.axis_index("dp"), 1, 0)
        own_member = own[:, None] == jnp.arange(buckets, dtype=jnp.int32)[None, :]
        own_peaks = jnp.max(jnp.where(own_member, peak_table, 0.0), axis=1, keepdims=True)
    unit = (exact / (own_peaks + epsilon)).astype(jnp.bfloat16)
    return unit.reshape(steps, 1, columns), peak_table, exact[steps - 1 :]


def solution(mesh):
    return jax.shard_map(
        functools.partial(on_device, mesh.shape["dp"], mesh.shape["tensor"]),
        mesh=mesh,
        in_specs=(P(None, "dp", None, "tensor"), P(None, "dp", None), P("dp", "tensor"), P(), P()),
        out_specs=(P(None, "dp", "tensor"), P(), P("dp", "tensor")),
        check_vma=False,
    )
```

time: 69.3 us -> 65 us (0.938)
  other arithmetic: 5.29 us -> 2.54 us
  local copies, waits for them, and re-layouts: 4.66 us -> 2.93 us
    convert_element_type x2 -> x0, other arithmetic: 1.71 us -> none  [the longest x1 1.05 us: on_device(): unit = (exact / (own_peaks[:, None, None] + epsilon)).astype(jnp.bfloat16)]
    reshape x2 -> x0, local copies, waits for them, and re-layouts: 1.39 us -> none  [the longest x1 0.75 us: on_device(): unit.reshape(steps, 1, columns)]
    eq x2 -> x0, other arithmetic: 1.39 us -> none  [the longest x1 0.73 us: on_device(): holds = arrival[:, None] == jnp.arange(rows, dtype=jnp.int32)[None, :]]
    slice x1, local copies, waits for them, and re-layouts: 0.79 us -> 1.67 us  [on_device(): return (unit.reshape(steps, 1, columns), peak_table, exact[steps - 1:])]
    add x1, other arithmetic: 0.01 us -> 0.79 us  [on_device(): unit = (exact / (own_peaks + epsilon)).astype(jnp.bfloat16)]
    exp2 x1 -> x0, other arithmetic: 0.69 us -> none  [on_device(): factors = jnp.exp2(-exponents[:, 0, :].astype(jnp.float32))]
    unnamed x4 -> x1, local copies, waits for them, and re-layouts: 1.61 us -> 1.26 us
where the time goes in v2:
time: 65 us; the launch traced here: 64.7 us
  Pallas kernels  58.6 us (90%)
  local copies, waits for them, and re-layouts  2.93 us (5%)
  other arithmetic  2.54 us (4%)
    pallas_call x1, Pallas kernels, on_device(): pl.pallas_call(functools.partial(exchange, n, orders, spans), out_shape=(...  58.6 us
    reshape x1, other arithmetic, on_device(): return (unit.reshape(steps, 1, columns), peak_table, exact[steps - 1:])  1.75 us
    slice x1, local copies, waits for them, and re-layouts, on_device(): return (unit.reshape(steps, 1, columns), peak_table, exact[steps - 1:])  1.67 us

profile of v2, /device:TPU:0, one launch (start us, length us, event | category | flops | bytes accessed | tf_op | source)
XLA Modules:
  0.0 64.7 jit_solution(2631162927087867603)
XLA Ops:
  0.6 58.6 %shard_map.76 = (f32[4,18432]{1,0:T(4,128)}, f32[4,16]{1,0:T(4,128)}, f32[4,128]{1,0:T(4,128)}) custom-call(bf16[4,1,32,18432]{3,2,1,0:T(8,128)(2,1)} %codes.1, s32[4,1,16]{2,1,0:T(1,128)} %exponents.1, bf16[1,18432]{1,0:T(2,128)(2,1)} %accumulated.1, s32[32]{0:T(128)} %arrival.1, s32[32]{0:T(128)} %bucket_of_row.1), custom_call_target="tpu_custom_call" | custom-call | tf_op jit(solution)/shard_map/pallas_call | solution.py:223
  59.3 0.8 %add_reduce_fusion = f32[4]{0:T(128)S(1)} fusion(f32[4,128]{1,0:T(4,128)} %get-tuple-element.7), kind=kLoop, calls=%fused_computation.2 | loop fusion | flops 4 | bytes 32 | tf_op jit(solution)/shard_map/add | solution.py:258
  60.1 1.7 %fusion = bf16[4,1,18432]{2,0,1:T(4,128)(2,1)} fusion(f32[4,18432]{1,0:T(4,128)} %get-tuple-element.6, f32[4]{0:T(128)S(1)} %add_reduce_fusion), kind=kLoop, calls=%fused_computation.1 | loop fusion | flops 147456 | bytes 442384 | tf_op jit(solution)/shard_map/reshape | solution.py:259
  61.8 1.7 %slice.7 = f32[1,18432]{1,0:T(1,128)} slice(f32[4,18432]{1,0:T(4,128)} %get-tuple-element.6), slice={[3:4], [0:18432]} | slice | bytes 147456 | tf_op jit(solution)/shard_map/slice | solution.py:259
  63.5 1.3 %copy.9 = f32[4,16]{1,0:T(4,128)} copy(f32[4,16]{1,0:T(4,128)} %get-tuple-element.13) | data formatting | bytes 512
